TPU v7x, 256 devices: a whole 4x4x8 slice. The times are simulated.
256 devices in a mesh: ctx: 16 (over y_hi, z), tp: 8 (over x, y_lo), probe: 2 (over core).
Axes of the slice: x: 4, y: 4 (y_hi: 2, y_lo: 2; y = y_hi * 2 + y_lo), z: 8, core: 2. Of those that a mesh axis runs over, the one named last changes fastest.
Arguments:
- latent: float32 [2048, 3072], P('ctx', 'tp'), may hold values from -6 to 6
- probes: int32 [2, 2048, 3072], P('probe', 'ctx', 'tp'), may hold values from 0 to 1
- modulation: float32 [2, 3, 3072], replicated, may hold values from -3 to 3
- pattern: int32 [16, 8], P('ctx'), may hold values from 0 to 15, as said below
- w_qkv: bfloat16 [3072, 3, 3072], P(None, None, 'tp'), may hold values from -0.109375 to 0.109375
- w_out: bfloat16 [3072, 3072], P('tp'), may hold values from -0.109375 to 0.109375
- w_up: bfloat16 [3072, 6144], P('ctx', 'tp'), may hold values from -0.109375 to 0.109375
- w_down: bfloat16 [6144, 3072], P('tp', 'ctx'), may hold values from -0.078125 to 0.078125
- q_gain: float32 [3072], P('tp'), may hold values from 0.5 to 5.1, as said below
- k_gain: float32 [3072], P('tp'), may hold values from 0.5 to 2
Outputs:
- latent_out: float32 [2048, 3072], P('ctx', 'tp')
- density_change: float32 [2048], P('ctx')
Inputs may be any that keep to these rules, and one draw needn't show every extreme that they name: `pattern`: row q lists key blocks for query block q: its first entry is q; the next entries are distinct blocks other than q up to a count of 1 to 8, after which every entry is q again; row 0 lists 8 distinct blocks. `q_gain`: positive gains.
All inputs are finite; a program needn't handle non-finite values.
Results may differ from a plain program's by a relative error of at most 0.034.
Values may be sent and summed in bfloat16 or wider, within the bound.
A program may use at most 128 MiB of HBM per device.

v0:
```python
from functools import partial
import math
import jax
import jax.numpy as jnp
from jax import lax
from jax.sharding import PartitionSpec as P

HD = 128
BLK = 128
K_SEL = 8
STEPS = 2
EPS = 1e-06
NEG_BIG = -1e30


def norm_features(rows, tangent, shift, stretch, full_width):
    row_sums = jnp.stack(
        [jnp.sum(rows, 1), jnp.sum(rows * rows, 1), jnp.sum(tangent, 1), jnp.sum(rows * tangent, 1)]
    )
    totals = lax.psum(row_sums, "tp")
    row_mean = totals[0][:, None] / full_width
    row_var = totals[1][:, None] / full_width - row_mean * row_mean
    tan_mean = totals[2][:, None] / full_width
    tan_var = 2.0 * (totals[3][:, None] / full_width - row_mean * tan_mean)
    inv_std = lax.rsqrt(row_var + EPS)
    centred = rows - row_mean
    normed = centred * inv_std
    tan_normed = (
        tangent - tan_mean
    ) * inv_std - 0.5 * centred * inv_std * inv_std * inv_std * tan_var
    normed_act = (normed * (1.0 + stretch) + shift).astype(jnp.bfloat16)
    tangent_act = (tan_normed * (1.0 + stretch)).astype(jnp.bfloat16)
    return (
        lax.all_gather(normed_act, "tp", axis=1, tiled=True),
        lax.all_gather(tangent_act, "tp", axis=1, tiled=True),
    )


def head_rms(projected, tan_projected, head_gain):
    row_count = projected.shape[0]
    heads_local = head_gain.shape[0] // HD
    head_view = projected.reshape(row_count, heads_local, HD)
    tan_view = tan_projected.reshape(row_count, heads_local, HD)
    gain_view = head_gain.reshape(heads_local, HD)
    inv_std = lax.rsqrt(jnp.mean(head_view * head_view, axis=-1, keepdims=True) + EPS)
    tan_inv = -inv_std * inv_std * inv_std * jnp.mean(head_view * tan_view, axis=-1, keepdims=True)
    result = (head_view * inv_std * gain_view).astype(jnp.bfloat16)
    tan_result = ((tan_view * inv_std + head_view * tan_inv) * gain_view).astype(jnp.bfloat16)
    return (result, tan_result)


def empty_carry(heads_local, row_count):
    return (
        jnp.full((heads_local, row_count), NEG_BIG, jnp.float32),
        jnp.zeros((heads_local, row_count), jnp.float32),
        jnp.zeros((heads_local, row_count, HD), jnp.float32),
        jnp.zeros((heads_local, row_count, HD), jnp.float32),
        jnp.zeros((heads_local, row_count), jnp.float32),
    )


def attend(state_carry, query, key_set, allowed):
    running_max, run_total, run_acc, tan_acc, tan_sum = state_carry
    q_rows, dq_rows = query
    k_rows, v_rows, dk_rows, dv_rows = key_set
    score_scale = 1.0 / math.sqrt(q_rows.shape[2])
    scores = (
        jnp.einsum("qhd,khd->hqk", q_rows, k_rows, preferred_element_type=jnp.float32) * score_scale
    )
    tan_scores = (
        jnp.einsum("qhd,khd->hqk", dq_rows, k_rows, preferred_element_type=jnp.float32)
        + jnp.einsum("qhd,khd->hqk", q_rows, dk_rows, preferred_element_type=jnp.float32)
    ) * score_scale
    key_mask = allowed[None, :, :]
    scores = jnp.where(key_mask, scores, NEG_BIG)
    new_max = jnp.maximum(running_max, jnp.max(scores, axis=2))
    weights = jnp.where(key_mask, jnp.exp(scores - new_max[:, :, None]), 0.0)
    values = v_rows.astype(jnp.float32)
    tan_values = dv_rows.astype(jnp.float32)
    weighted_ds = weights * tan_scores
    run_total = jnp.sum(weights, axis=2)
    run_acc = jnp.einsum("hqk,khd->hqd", weights, values, precision=lax.Precision.HIGHEST)
    tan_acc = jnp.einsum(
        "hqk,khd->hqd", weights, tan_values, precision=lax.Precision.HIGHEST
    ) + jnp.einsum("hqk,khd->hqd", weighted_ds, values, precision=lax.Precision.HIGHEST)
    tan_sum = jnp.sum(weighted_ds, axis=2)
    return (new_max, run_total, run_acc, tan_acc, tan_sum)


def finish(state_carry):
    running_max, run_total, run_acc, tan_acc, tan_sum = state_carry
    output = run_acc / run_total[:, :, None]
    tan_output = tan_acc / run_total[:, :, None] - (tan_sum / run_total)[:, :, None] * output
    heads_local, row_count, head_size = output.shape
    output = (
        output.transpose(1, 0, 2).reshape(row_count, heads_local * head_size).astype(jnp.bfloat16)
    )
    tan_output = (
        tan_output.transpose(1, 0, 2)
        .reshape(row_count, heads_local * head_size)
        .astype(jnp.bfloat16)
    )
    return (output, tan_output)


def select_blocks(whole_rows, chosen, block_total, heads_local):
    blocked = whole_rows.reshape(block_total, BLK, heads_local * HD)
    return jnp.take(blocked, chosen, axis=0).reshape(K_SEL * BLK, heads_local, HD)


def listed_attention(q_rows, dq_rows, whole_set, pattern, block_total, heads_local):
    chosen = pattern[0]
    valid_cols = (jnp.arange(K_SEL) == 0) | (chosen != chosen[0])
    allowed = jnp.broadcast_to(jnp.repeat(valid_cols, BLK)[None, :], (BLK, K_SEL * BLK))
    key_set = tuple(
        (select_blocks(member, chosen, block_total, heads_local) for member in whole_set)
    )
    query = (q_rows[0:BLK], dq_rows[0:BLK])
    block_out, block_tan = finish(attend(empty_carry(heads_local, BLK), query, key_set, allowed))
    return (block_out, block_tan)


def local(latent, probes, modulation, pattern, w_qkv, w_out, w_up, w_down, q_gain, k_gain):
    row_count, local_width = latent.shape
    full_width = local_width * lax.axis_size("tp")
    feature_start = lax.axis_index("tp") * local_width
    heads_local = q_gain.shape[0] // HD
    block_total = row_count * lax.axis_size("ctx") // BLK
    step_size = 1.0 / STEPS
    probe_signs = 2.0 * probes[0].astype(jnp.float32) - 1.0
    up_full, down_full = (
        lax.all_gather(w_up, "ctx", axis=0, tiled=True),
        lax.all_gather(w_down, "ctx", axis=1, tiled=True),
    )
    gelu_tanh = partial(jax.nn.gelu, approximate=True)
    change = jnp.zeros((row_count,), jnp.float32)
    for euler_step in range(STEPS):
        mod_local = lax.dynamic_slice_in_dim(modulation[euler_step], feature_start, local_width, 1)
        normed_act, tangent_act = norm_features(
            latent, probe_signs, mod_local[0], mod_local[1], full_width
        )
        stacked = jnp.concatenate([normed_act, tangent_act], axis=0)
        projected = jnp.einsum("rd,dcf->crf", stacked, w_qkv, preferred_element_type=jnp.float32)
        q_rows, dq_rows = head_rms(projected[0, :row_count], projected[0, row_count:], q_gain)
        k_heads, dk_heads = head_rms(projected[1, :row_count], projected[1, row_count:], k_gain)
        k_rows = k_heads.reshape(row_count, heads_local * HD)
        dk_rows = dk_heads.reshape(row_count, heads_local * HD)
        v_rows = projected[2, :row_count].astype(jnp.bfloat16)
        dv_rows = projected[2, row_count:].astype(jnp.bfloat16)
        k_whole, v_whole, dk_whole, dv_whole = (
            lax.all_gather(k_rows, "ctx", axis=0, tiled=True),
            lax.all_gather(v_rows, "ctx", axis=0, tiled=True),
            lax.all_gather(dk_rows, "ctx", axis=0, tiled=True),
            lax.all_gather(dv_rows, "ctx", axis=0, tiled=True),
        )
        attended, tan_attended = listed_attention(
            q_rows,
            dq_rows,
            (k_whole, v_whole, dk_whole, dv_whole),
            pattern,
            block_total,
            heads_local,
        )
        pre_hidden = jnp.dot(stacked, up_full, preferred_element_type=jnp.float32)
        hidden, tan_hidden = jax.jvp(
            gelu_tanh, (pre_hidden[:row_count],), (pre_hidden[row_count:],)
        )
        attn_rows = jnp.concatenate([attended, tan_attended], axis=0)
        mlp_rows = jnp.concatenate(
            [hidden.astype(jnp.bfloat16), tan_hidden.astype(jnp.bfloat16)], axis=0
        )
        partials = jnp.dot(attn_rows, w_out, preferred_element_type=jnp.float32) + jnp.dot(
            mlp_rows, down_full, preferred_element_type=jnp.float32
        )
        summed = lax.psum_scatter(
            partials.astype(jnp.bfloat16), "tp", scatter_dimension=1, tiled=True
        ).astype(jnp.float32)
        speed = mod_local[2] * summed[:row_count]
        tan_speed = mod_local[2] * summed[row_count:]
        change = change + jnp.sum(probe_signs * tan_speed, axis=1)
        latent = latent + step_size * speed
    total_change = lax.psum(change, ("tp", "probe"))
    density_change = -step_size * total_change / (lax.axis_size("probe") * math.sqrt(full_width))
    return (latent, density_change)


def solution(mesh):
    return jax.shard_map(
        local,
        mesh=mesh,
        in_specs=(
            P("ctx", "tp"),
            P("probe", "ctx", "tp"),
            P(),
            P("ctx", None),
            P(None, None, "tp"),
            P("tp", None),
            P("ctx", "tp"),
            P("tp", "ctx"),
            P("tp"),
            P("tp"),
        ),
        out_specs=(P("ctx", "tp"), P("ctx")),
        check_vma=False,
    )
```

profile of v0, /device:TPU:1, one launch (start us, length us, event | category | flops | bytes accessed | tf_op | source)
XLA Modules:
  0.0 1214.0 jit_solution(16724503533342251219)
XLA Ops:
  9.6 16.8 %psum.21 = f32[4,128]{1,0:T(4,128)S(1)} all-reduce(f32[4,128]{1,0:T(4,128)S(1)} %fusion.105), channel_id=1, replica_groups=mesh['ctx'=16,'tp'=8,'probe'=2] {'tp'}, use_global_device_ids=true, to_apply=%region_4.0 | all-reduce | flops 512 | bytes 4096 | tf_op jit(solution)/shard_map/psum | solution.py:20
  26.4 1.6 fusion.134
  29.3 25.0 %all_gather.43 = bf16[128,3072]{1,0:T(8,128)(2,1)S(1)} all-gather(bf16[128,384]{1,0:T(8,128)(2,1)S(1)} %get-tuple-element.49), channel_id=1, replica_groups=mesh['ctx'=16,'tp'=8,'probe'=2] {'tp'}, dimensions={1}, use_global_device_ids=true | all-gather | bytes 884736 | tf_op jit(solution)/shard_map/all_gather | solution.py:35
  54.4 24.5 %all_gather.42 = bf16[128,3072]{1,0:T(8,128)(2,1)S(1)} all-gather(bf16[128,384]{1,0:T(8,128)(2,1)S(1)} %get-tuple-element.50), channel_id=1, replica_groups=mesh['ctx'=16,'tp'=8,'probe'=2] {'tp'}, dimensions={1}, use_global_device_ids=true | all-gather | bytes 884736 | tf_op jit(solution)/shard_map/all_gather | solution.py:34
  79.0 5.8 fusion.135
  87.3 1.8 copy.102
  89.0 1.7 copy.91
  91.7 1.5 reduce_sum.202
  94.6 1.7 copy.103
  97.0 1.7 copy.92
  98.8 1.7 fusion.83
  105.8 74.2 %all-gather.27.cloned.1.call-done = bf16[1,2048,384]{2,1,0:T(8,128)(2,1)} async-done(((bf16[1,128,384]{2,1,0:T(8,128)(2,1)}), bf16[1,2048,384]{2,1,0:T(8,128)(2,1)}) %all-gather.27.cloned.1.call-update) | async-done | bytes 1572880 | tf_op jit(solution)/shard_map/all_gather | solution.py:152
  180.0 2.1 gather_fusion.1
  182.1 79.4 %all-gather.29.cloned.1.call-done = bf16[1,2048,384]{2,1,0:T(8,128)(2,1)} async-done(((bf16[1,128,384]{2,1,0:T(8,128)(2,1)}), bf16[1,2048,384]{2,1,0:T(8,128)(2,1)}) %all-gather.29.cloned.1.call-update) | async-done | bytes 1572880 | tf_op jit(solution)/shard_map/all_gather | solution.py:154
  261.5 3.0 gather_fusion.2
  264.5 79.1 %all-gather.17.cloned.1.call-done = bf16[2048,384]{1,0:T(8,128)(2,1)} async-done(((bf16[128,384]{1,0:T(8,128)(2,1)}), bf16[2048,384]{1,0:T(8,128)(2,1)}) %all-gather.17.cloned.1.call-update) | async-done | bytes 1572880 | tf_op jit(solution)/shard_map/all_gather | solution.py:153
  343.6 2.9 gather_fusion.3
  346.5 78.4 %all-gather.15.cloned.1.call-done = bf16[2048,384]{1,0:T(8,128)(2,1)} async-done(((bf16[128,384]{1,0:T(8,128)(2,1)}), bf16[2048,384]{1,0:T(8,128)(2,1)}) %all-gather.15.cloned.1.call-update) | async-done | bytes 1572880 | tf_op jit(solution)/shard_map/all_gather | solution.py:151
  424.9 3.0 gather_fusion
  427.9 3.4 broadcast_select_fusion.6
  431.4 1.6 copy.96
  433.0 1.2 reshape.365
  434.2 2.5 copy.97
  436.8 2.2 reshape.367
  438.9 1.4 copy.93
  440.3 1.4 reshape.363
  441.7 3.2 reshape.476
  451.8 76.6 %all-gather.19.cloned.1.call-done = bf16[3072,768]{1,0:T(8,128)(2,1)} async-done(((bf16[192,768]{1,0:T(8,128)(2,1)}), bf16[3072,768]{1,0:T(8,128)(2,1)}) %all-gather.19.cloned.1.call-update) | async-done | bytes 4718608 | tf_op jit(solution)/shard_map/all_gather | solution.py:132
  528.4 4.2 fusion.143
  532.9 98.5 %all-gather.21.cloned.1.call-done = bf16[768,3072]{0,1:T(8,128)(2,1)} async-done(((bf16[768,192]{0,1:T(8,128)(2,1)}), bf16[768,3072]{0,1:T(8,128)(2,1)}) %all-gather.21.cloned.1.call-update) | async-done | bytes 4718608 | tf_op jit(solution)/shard_map/all_gather | solution.py:133
  631.3 3.7 fusion.54
  635.1 2.2 fusion
  637.2 2.6 copy.142
  639.9 1.4 dynamic-slice_reduce_fusion.1
  641.3 42.1 %reduce-scatter.7.cloned.1.call-done = bf16[384,256]{1,0:T(8,128)(2,1)} async-done(((bf16[3072,256]{1,0:T(8,128)(2,1)}), bf16[384,256]{1,0:T(8,128)(2,1)}) %reduce-scatter.7.cloned.1.call-update) | async-done | bytes 196624
  684.7 14.6 %psum.22 = f32[4,128]{1,0:T(4,128)S(1)} all-reduce(f32[4,128]{1,0:T(4,128)S(1)} %fusion.106), channel_id=1, replica_groups=mesh['ctx'=16,'tp'=8,'probe'=2] {'tp'}, use_global_device_ids=true, to_apply=%region_16.18 | all-reduce | flops 512 | bytes 4096 | tf_op jit(solution)/shard_map/psum | solution.py:20
  699.6 24.3 %all_gather.51 = bf16[128,3072]{1,0:T(8,128)(2,1)S(1)} all-gather(bf16[128,384]{1,0:T(8,128)(2,1)S(1)} %get-tuple-element.47), channel_id=1, replica_groups=mesh['ctx'=16,'tp'=8,'probe'=2] {'tp'}, dimensions={1}, use_global_device_ids=true | all-gather | bytes 884736 | tf_op jit(solution)/shard_map/all_gather | solution.py:35
  723.8 24.5 %all_gather.50 = bf16[128,3072]{1,0:T(8,128)(2,1)S(1)} all-gather(bf16[128,384]{1,0:T(8,128)(2,1)S(1)} %get-tuple-element.48), channel_id=1, replica_groups=mesh['ctx'=16,'tp'=8,'probe'=2] {'tp'}, dimensions={1}, use_global_device_ids=true | all-gather | bytes 884736 | tf_op jit(solution)/shard_map/all_gather | solution.py:34
  748.4 6.8 fusion.139
  756.8 2.0 slice_multiply_fusion.4
  759.4 1.8 fusion.78
  763.9 4.3 fusion.144
  768.6 3.1 fusion.58
  771.6 79.8 %all-gather.31.cloned.1.call-done = bf16[1,2048,384]{2,1,0:T(8,128)(2,1)} async-done(((bf16[1,128,384]{2,1,0:T(8,128)(2,1)}), bf16[1,2048,384]{2,1,0:T(8,128)(2,1)}) %all-gather.31.cloned.1.call-update) | async-done | bytes 1572880 | tf_op jit(solution)/shard_map/all_gather | solution.py:152
  851.4 2.2 gather_fusion.5
  853.6 79.3 %all-gather.33.cloned.1.call-done = bf16[1,2048,384]{2,1,0:T(8,128)(2,1)} async-done(((bf16[1,128,384]{2,1,0:T(8,128)(2,1)}), bf16[1,2048,384]{2,1,0:T(8,128)(2,1)}) %all-gather.33.cloned.1.call-update) | async-done | bytes 1572880 | tf_op jit(solution)/shard_map/all_gather | solution.py:154
  932.9 3.1 gather_fusion.6
  936.0 78.3 %all-gather.25.cloned.1.call-done = bf16[2048,384]{1,0:T(8,128)(2,1)} async-done(((bf16[128,384]{1,0:T(8,128)(2,1)}), bf16[2048,384]{1,0:T(8,128)(2,1)}) %all-gather.25.cloned.1.call-update) | async-done | bytes 1572880 | tf_op jit(solution)/shard_map/all_gather | solution.py:153
  1014.2 3.1 gather_fusion.7
  1017.3 78.4 %all-gather.23.cloned.1.call-done = bf16[2048,384]{1,0:T(8,128)(2,1)} async-done(((bf16[128,384]{1,0:T(8,128)(2,1)}), bf16[2048,384]{1,0:T(8,128)(2,1)}) %all-gather.23.cloned.1.call-update) | async-done | bytes 1572880 | tf_op jit(solution)/shard_map/all_gather | solution.py:151
  1095.8 3.1 gather_fusion.4
  1098.8 3.5 broadcast_select_fusion.2
  1102.3 2.5 copy.113
  1104.9 2.2 reshape.373
  1107.0 1.3 copy.110
  1108.4 1.4 reshape.371
  1109.8 2.4 copy.114
  1112.2 2.2 reshape.375
  1114.4 3.2 reshape.477
  1124.2 2.2 fusion.1
  1126.4 2.6 copy.144
  1129.1 44.3 %reduce-scatter.9.cloned.1.call-done = bf16[384,256]{1,0:T(8,128)(2,1)} async-done(((bf16[3072,256]{1,0:T(8,128)(2,1)}), bf16[384,256]{1,0:T(8,128)(2,1)}) %reduce-scatter.9.cloned.1.call-update) | async-done | bytes 196624
  1174.5 1.7 fusion.63
  1176.2 30.4 %psum.23 = f32[128]{0:T(128)S(1)} all-reduce(f32[128]{0:T(128)S(1)} %add.227), channel_id=1, replica_groups=mesh['ctx'=16,'tp'=8,'probe'=2] {'tp','probe'}, use_global_device_ids=true, to_apply=%region_27.29 | all-reduce | flops 128 | bytes 1024 | tf_op jit(solution)/shard_map/psum | solution.py:182
  (157 shorter events, 36.3 us)
Async XLA Ops:
  7.2 627.9 %copy-start = (bf16[384,3072]{1,0:T(8,128)(2,1)S(1)}, bf16[384,3072]{1,0:T(8,128)(2,1)}, u32[]{:S(2)}) copy-start(bf16[384,3072]{1,0:T(8,128)(2,1)} %param.17) | copy-start | bytes 7077892
  7.2 172.8 %all-gather.27.cloned.1.call-start = ((), (), s32[]{:S(2)}) async-start(), calls=%async_computation.8 | async-start | bytes 1671168 | tf_op jit(solution)/shard_map/all_gather | solution.py:152
  8.4 1.2 copy-start.26
  79.0 5.8 copy-start.17
  85.6 175.9 %all-gather.29.cloned.1.call-start = ((), (), s32[]{:S(2)}) async-start(), calls=%async_computation.9 | async-start | bytes 1671168 | tf_op jit(solution)/shard_map/all_gather | solution.py:154
  86.3 257.3 %all-gather.17.cloned.1.call-start = ((), (), s32[]{:S(2)}) async-start(), calls=%async_computation.3 | async-start | bytes 1671168 | tf_op jit(solution)/shard_map/all_gather | solution.py:153
  87.3 11.5 copy-start.21
  96.3 8.1 copy-start.28
  100.5 324.4 %all-gather.15.cloned.1.call-start = ((), (), s32[]{:S(2)}) async-start(), calls=%async_computation.2 | async-start | bytes 1671168 | tf_op jit(solution)/shard_map/all_gather | solution.py:151
  101.1 427.2 %all-gather.19.cloned.1.call-start = ((), (), s32[]{:S(2)}) async-start(), calls=%async_computation.4 | async-start | bytes 5013504 | tf_op jit(solution)/shard_map/all_gather | solution.py:132
  101.7 529.6 %all-gather.21.cloned.1.call-start = ((), (), s32[]{:S(2)}) async-start(), calls=%async_computation.5 | async-start | bytes 5013504 | tf_op jit(solution)/shard_map/all_gather | solution.py:133
  102.3 581.1 %reduce-scatter.7.cloned.1.call-start = ((), (), s32[]{:S(2)}) async-start(), calls=%async_computation.12 | async-start | bytes 1769472
  104.5 320.5 %copy-start.20 = (s32[1024]{0:T(1024)}, s32[1024]{0:T(1024)S(1)}, u32[]{:S(2)}) copy-start(s32[1024]{0:T(1024)S(1)} %pad_clamp_fusion) | copy-start | bytes 12292
  434.2 4.7 copy-start.5
  440.3 4.7 copy-start.19
  445.0 1.0 copy-start.25
  446.0 1.2 copy-start.4
  447.2 1.1 copy-start.15
  448.1 1.5 copy-start.8
  639.8 44.7 %copy-start.2 = (s32[1,128,384]{2,1,0:T(8,128)S(1)}, s32[1,128,384]{2,1,0:T(8,128)}, u32[]{:S(2)}) copy-start(s32[1,128,384]{2,1,0:T(8,128)} %param.13) | copy-start | bytes 589828
  639.8 44.7 %copy-start.11 = (f32[128,384]{1,0:T(8,128)S(1)}, f32[128,384]{1,0:T(8,128)}, u32[]{:S(2)}) copy-start(f32[128,384]{1,0:T(8,128)} %param.12) | copy-start | bytes 589828
  639.8 44.9 %copy-start.27 = (f32[128]{0:T(128)S(1)}, f32[128]{0:T(128)}, u32[]{:S(2)}) copy-start(f32[128]{0:T(128)} %copy-done.26) | copy-start | bytes 1540
  639.9 211.5 %all-gather.31.cloned.1.call-start = ((), (), s32[]{:S(2)}) async-start(), calls=%async_computation.10 | async-start | bytes 1671168 | tf_op jit(solution)/shard_map/all_gather | solution.py:152
  684.5 63.8 %copy-start.14 = (f32[256,384]{1,0:T(8,128)}, f32[256,384]{1,0:T(8,128)S(1)}, u32[]{:S(2)}) copy-start(f32[256,384]{1,0:T(8,128)S(1)} %convert_element_type.128) | copy-start | bytes 1179652
  684.7 63.6 %copy-start.12 = (f32[128,384]{1,0:T(8,128)}, f32[128,384]{1,0:T(8,128)S(1)}, u32[]{:S(2)}) copy-start(f32[128,384]{1,0:T(8,128)S(1)} %get-tuple-element.23) | copy-start | bytes 589828
  748.4 6.8 copy-start.18
  756.0 176.9 %all-gather.33.cloned.1.call-start = ((), (), s32[]{:S(2)}) async-start(), calls=%async_computation.11 | async-start | bytes 1671168 | tf_op jit(solution)/shard_map/all_gather | solution.py:154
  756.7 257.5 %all-gather.25.cloned.1.call-start = ((), (), s32[]{:S(2)}) async-start(), calls=%async_computation.7 | async-start | bytes 1671168 | tf_op jit(solution)/shard_map/all_gather | solution.py:153
  758.7 0.7 copy-start.22
  761.2 334.6 %all-gather.23.cloned.1.call-start = ((), (), s32[]{:S(2)}) async-start(), calls=%async_computation.6 | async-start | bytes 1671168 | tf_op jit(solution)/shard_map/all_gather | solution.py:151
  761.9 411.4 %reduce-scatter.9.cloned.1.call-start = ((), (), s32[]{:S(2)}) async-start(), calls=%async_computation.13 | async-start | bytes 1769472
  762.1 6.2 copy-start.9
  762.1 6.4 slice-start
  763.9 4.7 slice-start.1
  1102.3 4.7 copy-start.6
  1117.6 0.9 copy-start.10
  1117.6 0.9 copy-start.24
  1118.6 1.1 copy-start.16
  1119.7 1.2 copy-start.3
  1120.9 1.1 copy-start.7
  1122.1 2.1 copy-start.1
  1129.0 45.4 %copy-start.13 = (f32[128,384]{1,0:T(8,128)S(1)}, f32[128,384]{1,0:T(8,128)}, u32[]{:S(2)}) copy-start(f32[128,384]{1,0:T(8,128)} %copy-done.12) | copy-start | bytes 589828
  1129.0 45.4 %copy-start.23 = (f32[384]{0:T(512)S(1)}, f32[384]{0:T(512)}, u32[]{:S(2)}) copy-start(f32[384]{0:T(512)} %get-tuple-element.15) | copy-start | bytes 4612
Sparse Core Ops, SparseCore 0:
  85.7 94.2 all-gather.26
  182.6 78.8 all-gather.28
  264.7 78.8 all-gather.16
  346.0 78.8 all-gather.14
  427.4 100.9 all-gather.18
  530.8 100.4 all-gather.20
  640.0 43.3 reduce-scatter.6
  756.1 95.2 all-gather.30
  854.0 78.8 all-gather.32
  935.3 78.8 all-gather.24
  1016.8 78.8 all-gather.22
  1129.2 44.1 reduce-scatter.8
where the time goes:
time: 1220 us; the launch traced here: 1210 us
  waiting for transfers between devices  892 us (73%)
  blocking collectives  160 us (13%)
  local copies, waits for them, and re-layouts  76.3 us (6%)
  matrix products  42.8 us (4%)
  other arithmetic  27.4 us (2%)
  between operations  14.8 us (1%)
    all_gather x2, waiting for transfers between devices, local(): lax.all_gather(dv_rows, 'ctx', axis=0, tiled=True)  159 us
    all_gather x2, waiting for transfers between devices, local(): lax.all_gather(dk_rows, 'ctx', axis=0, tiled=True)  157 us
    all_gather x2, waiting for transfers between devices, local(): lax.all_gather(k_rows, 'ctx', axis=0, tiled=True)  157 us
    all_gather x2, waiting for transfers between devices, local(): lax.all_gather(v_rows, 'ctx', axis=0, tiled=True)  154 us
    all_gather x1, waiting for transfers between devices, local(): lax.all_gather(w_down, 'ctx', axis=1, tiled=True)  98.5 us
    unnamed x14, waiting for transfers between devices  90.1 us
    all_gather x1, waiting for transfers between devices, local(): lax.all_gather(w_up, 'ctx', axis=0, tiled=True)  76.6 us
    all_gather x2, blocking collectives, norm_features(): lax.all_gather(tangent_act, 'tp', axis=1, tiled=True)  49.3 us
  transfers between devices with their start and end apart: 12, of which 12 were waited for; matrix products, arithmetic and copies ran while one was open for 7% of the time, Pallas kernels for 0%

commit v1 on v0

--- a/solution.py
+++ b/solution.py
@@ -179,7 +179,7 @@
         tan_speed = mod_local[2] * summed[row_count:]
         change = change + jnp.sum(probe_signs * tan_speed, axis=1)
         latent = latent + step_size * speed
-    total_change = lax.psum(change, ("tp", "probe"))
+    total_change = lax.psum(lax.psum(change, "probe"), "tp")
     density_change = -step_size * total_change / (lax.axis_size("probe") * math.sqrt(full_width))
     return (latent, density_change)
 

time: 1220 us -> 1210 us (level)
    psum x1 -> x2, blocking collectives: 30.4 us -> 20 us  [local(): total_change = lax.psum(lax.psum(change, 'probe'), 'tp')]
where the time goes in v1:
time: 1210 us; the launch traced here: 1200 us
  waiting for transfers between devices  893 us (74%)
  blocking collectives  150 us (12%)
  local copies, waits for them, and re-layouts  76.3 us (6%)
  matrix products  42.8 us (4%)
  other arithmetic  27.5 us (2%)
  between operations  14.8 us (1%)
    all_gather x2, waiting for transfers between devices, local(): lax.all_gather(dv_rows, 'ctx', axis=0, tiled=True)  159 us
    all_gather x2, waiting for transfers between devices, local(): lax.all_gather(dk_rows, 'ctx', axis=0, tiled=True)  157 us
    all_gather x2, waiting for transfers between devices, local(): lax.all_gather(k_rows, 'ctx', axis=0, tiled=True)  157 us
    all_gather x2, waiting for transfers between devices, local(): lax.all_gather(v_rows, 'ctx', axis=0, tiled=True)  154 us
    all_gather x1, waiting for transfers between devices, local(): lax.all_gather(w_down, 'ctx', axis=1, tiled=True)  98.5 us
    unnamed x14, waiting for transfers between devices  90.3 us
    all_gather x1, waiting for transfers between devices, local(): lax.all_gather(w_up, 'ctx', axis=0, tiled=True)  76.6 us
    all_gather x2, blocking collectives, norm_features(): lax.all_gather(tangent_act, 'tp', axis=1, tiled=True)  49.3 us
  transfers between devices with their start and end apart: 12, of which 12 were waited for; matrix products, arithmetic and copies ran while one was open for 7% of the time, Pallas kernels for 0%

profile of v1, /device:TPU:1, one launch (start us, length us, event | category | flops | bytes accessed | tf_op | source)
XLA Modules:
  0.0 1204.0 jit_solution(18139537616674505476)
XLA Ops:
  9.6 16.8 %psum.28 = f32[4,128]{1,0:T(4,128)S(1)} all-reduce(f32[4,128]{1,0:T(4,128)S(1)} %fusion.105), channel_id=1, replica_groups=mesh['ctx'=16,'tp'=8,'probe'=2] {'tp'}, use_global_device_ids=true, to_apply=%region_4.0 | all-reduce | flops 512 | bytes 4096 | tf_op jit(solution)/shard_map/psum | solution.py:20
  26.4 1.6 fusion.134
  29.3 25.0 %all_gather.43 = bf16[128,3072]{1,0:T(8,128)(2,1)S(1)} all-gather(bf16[128,384]{1,0:T(8,128)(2,1)S(1)} %get-tuple-element.49), channel_id=1, replica_groups=mesh['ctx'=16,'tp'=8,'probe'=2] {'tp'}, dimensions={1}, use_global_device_ids=true | all-gather | bytes 884736 | tf_op jit(solution)/shard_map/all_gather | solution.py:35
  54.3 24.5 %all_gather.42 = bf16[128,3072]{1,0:T(8,128)(2,1)S(1)} all-gather(bf16[128,384]{1,0:T(8,128)(2,1)S(1)} %get-tuple-element.50), channel_id=1, replica_groups=mesh['ctx'=16,'tp'=8,'probe'=2] {'tp'}, dimensions={1}, use_global_device_ids=true | all-gather | bytes 884736 | tf_op jit(solution)/shard_map/all_gather | solution.py:34
  79.0 5.8 fusion.135
  87.3 1.7 copy.102
  89.0 1.7 copy.91
  91.7 1.5 reduce_sum.202
  94.6 1.7 copy.103
  97.0 1.7 copy.92
  98.8 1.7 fusion.83
  105.8 74.3 %all-gather.27.cloned.1.call-done = bf16[1,2048,384]{2,1,0:T(8,128)(2,1)} async-done(((bf16[1,128,384]{2,1,0:T(8,128)(2,1)}), bf16[1,2048,384]{2,1,0:T(8,128)(2,1)}) %all-gather.27.cloned.1.call-update) | async-done | bytes 1572880 | tf_op jit(solution)/shard_map/all_gather | solution.py:152
  180.0 2.1 gather_fusion.1
  182.1 79.4 %all-gather.29.cloned.1.call-done = bf16[1,2048,384]{2,1,0:T(8,128)(2,1)} async-done(((bf16[1,128,384]{2,1,0:T(8,128)(2,1)}), bf16[1,2048,384]{2,1,0:T(8,128)(2,1)}) %all-gather.29.cloned.1.call-update) | async-done | bytes 1572880 | tf_op jit(solution)/shard_map/all_gather | solution.py:154
  261.5 3.0 gather_fusion.2
  264.5 79.1 %all-gather.17.cloned.1.call-done = bf16[2048,384]{1,0:T(8,128)(2,1)} async-done(((bf16[128,384]{1,0:T(8,128)(2,1)}), bf16[2048,384]{1,0:T(8,128)(2,1)}) %all-gather.17.cloned.1.call-update) | async-done | bytes 1572880 | tf_op jit(solution)/shard_map/all_gather | solution.py:153
  343.6 3.0 gather_fusion.3
  346.5 78.4 %all-gather.15.cloned.1.call-done = bf16[2048,384]{1,0:T(8,128)(2,1)} async-done(((bf16[128,384]{1,0:T(8,128)(2,1)}), bf16[2048,384]{1,0:T(8,128)(2,1)}) %all-gather.15.cloned.1.call-update) | async-done | bytes 1572880 | tf_op jit(solution)/shard_map/all_gather | solution.py:151
  425.0 3.0 gather_fusion
  427.9 3.5 broadcast_select_fusion.6
  431.4 1.6 copy.96
  434.2 2.6 copy.97
  436.8 2.2 reshape.367
  439.0 1.4 copy.93
  440.3 1.4 reshape.363
  441.8 3.2 reshape.476
  451.8 76.6 %all-gather.19.cloned.1.call-done = bf16[3072,768]{1,0:T(8,128)(2,1)} async-done(((bf16[192,768]{1,0:T(8,128)(2,1)}), bf16[3072,768]{1,0:T(8,128)(2,1)}) %all-gather.19.cloned.1.call-update) | async-done | bytes 4718608 | tf_op jit(solution)/shard_map/all_gather | solution.py:132
  528.4 4.2 fusion.143
  532.9 98.5 %all-gather.21.cloned.1.call-done = bf16[768,3072]{0,1:T(8,128)(2,1)} async-done(((bf16[768,192]{0,1:T(8,128)(2,1)}), bf16[768,3072]{0,1:T(8,128)(2,1)}) %all-gather.21.cloned.1.call-update) | async-done | bytes 4718608 | tf_op jit(solution)/shard_map/all_gather | solution.py:133
  631.3 3.7 fusion.54
  635.1 2.1 fusion
  637.2 2.6 copy.142
  639.9 1.4 dynamic-slice_reduce_fusion.1
  641.3 42.1 %reduce-scatter.7.cloned.1.call-done = bf16[384,256]{1,0:T(8,128)(2,1)} async-done(((bf16[3072,256]{1,0:T(8,128)(2,1)}), bf16[384,256]{1,0:T(8,128)(2,1)}) %reduce-scatter.7.cloned.1.call-update) | async-done | bytes 196624
  684.8 14.6 %psum.29 = f32[4,128]{1,0:T(4,128)S(1)} all-reduce(f32[4,128]{1,0:T(4,128)S(1)} %fusion.106), channel_id=1, replica_groups=mesh['ctx'=16,'tp'=8,'probe'=2] {'tp'}, use_global_device_ids=true, to_apply=%region_16.18 | all-reduce | flops 512 | bytes 4096 | tf_op jit(solution)/shard_map/psum | solution.py:20
  699.6 24.3 %all_gather.51 = bf16[128,3072]{1,0:T(8,128)(2,1)S(1)} all-gather(bf16[128,384]{1,0:T(8,128)(2,1)S(1)} %get-tuple-element.47), channel_id=1, replica_groups=mesh['ctx'=16,'tp'=8,'probe'=2] {'tp'}, dimensions={1}, use_global_device_ids=true | all-gather | bytes 884736 | tf_op jit(solution)/shard_map/all_gather | solution.py:35
  723.8 24.3 %all_gather.50 = bf16[128,3072]{1,0:T(8,128)(2,1)S(1)} all-gather(bf16[128,384]{1,0:T(8,128)(2,1)S(1)} %get-tuple-element.48), channel_id=1, replica_groups=mesh['ctx'=16,'tp'=8,'probe'=2] {'tp'}, dimensions={1}, use_global_device_ids=true | all-gather | bytes 884736 | tf_op jit(solution)/shard_map/all_gather | solution.py:34
  748.3 6.8 fusion.139
  756.6 2.0 slice_multiply_fusion.4
  759.3 1.8 fusion.78
  763.8 4.3 fusion.144
  768.5 3.1 fusion.58
  771.5 80.1 %all-gather.31.cloned.1.call-done = bf16[1,2048,384]{2,1,0:T(8,128)(2,1)} async-done(((bf16[1,128,384]{2,1,0:T(8,128)(2,1)}), bf16[1,2048,384]{2,1,0:T(8,128)(2,1)}) %all-gather.31.cloned.1.call-update) | async-done | bytes 1572880 | tf_op jit(solution)/shard_map/all_gather | solution.py:152
  851.7 2.2 gather_fusion.5
  853.9 79.3 %all-gather.33.cloned.1.call-done = bf16[1,2048,384]{2,1,0:T(8,128)(2,1)} async-done(((bf16[1,128,384]{2,1,0:T(8,128)(2,1)}), bf16[1,2048,384]{2,1,0:T(8,128)(2,1)}) %all-gather.33.cloned.1.call-update) | async-done | bytes 1572880 | tf_op jit(solution)/shard_map/all_gather | solution.py:154
  933.2 3.1 gather_fusion.6
  936.2 78.3 %all-gather.25.cloned.1.call-done = bf16[2048,384]{1,0:T(8,128)(2,1)} async-done(((bf16[128,384]{1,0:T(8,128)(2,1)}), bf16[2048,384]{1,0:T(8,128)(2,1)}) %all-gather.25.cloned.1.call-update) | async-done | bytes 1572880 | tf_op jit(solution)/shard_map/all_gather | solution.py:153
  1014.5 3.1 gather_fusion.7
  1017.6 78.4 %all-gather.23.cloned.1.call-done = bf16[2048,384]{1,0:T(8,128)(2,1)} async-done(((bf16[128,384]{1,0:T(8,128)(2,1)}), bf16[2048,384]{1,0:T(8,128)(2,1)}) %all-gather.23.cloned.1.call-update) | async-done | bytes 1572880 | tf_op jit(solution)/shard_map/all_gather | solution.py:151
  1096.0 3.1 gather_fusion.4
  1099.1 3.5 broadcast_select_fusion.2
  1102.6 2.5 copy.113
  1105.2 2.2 reshape.373
  1107.3 1.3 copy.110
  1108.6 1.4 reshape.371
  1110.1 2.4 copy.114
  1112.5 2.2 reshape.375
  1114.7 3.2 reshape.477
  1124.5 2.2 fusion.1
  1126.7 2.6 copy.144
  1129.3 44.4 %reduce-scatter.9.cloned.1.call-done = bf16[384,256]{1,0:T(8,128)(2,1)} async-done(((bf16[3072,256]{1,0:T(8,128)(2,1)}), bf16[384,256]{1,0:T(8,128)(2,1)}) %reduce-scatter.9.cloned.1.call-update) | async-done | bytes 196624
  1174.9 1.7 fusion.63
  1176.6 5.7 psum.30
  1182.3 14.3 %psum.31 = f32[128]{0:T(128)S(1)} all-reduce(f32[128]{0:T(128)S(1)} %psum.30), channel_id=1, replica_groups=mesh['ctx'=16,'tp'=8,'probe'=2] {'tp'}, use_global_device_ids=true, to_apply=%region_28.30 | all-reduce | flops 128 | bytes 1024 | tf_op jit(solution)/shard_map/psum | solution.py:182
  (158 shorter events, 37.5 us)
Async XLA Ops:
  7.2 627.9 %copy-start = (bf16[384,3072]{1,0:T(8,128)(2,1)S(1)}, bf16[384,3072]{1,0:T(8,128)(2,1)}, u32[]{:S(2)}) copy-start(bf16[384,3072]{1,0:T(8,128)(2,1)} %param.17) | copy-start | bytes 7077892
  7.2 172.8 %all-gather.27.cloned.1.call-start = ((), (), s32[]{:S(2)}) async-start(), calls=%async_computation.8 | async-start | bytes 1671168 | tf_op jit(solution)/shard_map/all_gather | solution.py:152
  8.4 1.2 copy-start.26
  79.0 5.8 copy-start.17
  85.6 175.9 %all-gather.29.cloned.1.call-start = ((), (), s32[]{:S(2)}) async-start(), calls=%async_computation.9 | async-start | bytes 1671168 | tf_op jit(solution)/shard_map/all_gather | solution.py:154
  86.3 257.3 %all-gather.17.cloned.1.call-start = ((), (), s32[]{:S(2)}) async-start(), calls=%async_computation.3 | async-start | bytes 1671168 | tf_op jit(solution)/shard_map/all_gather | solution.py:153
  87.3 11.5 copy-start.21
  96.3 8.1 copy-start.28
  100.5 324.4 %all-gather.15.cloned.1.call-start = ((), (), s32[]{:S(2)}) async-start(), calls=%async_computation.2 | async-start | bytes 1671168 | tf_op jit(solution)/shard_map/all_gather | solution.py:151
  101.1 427.2 %all-gather.19.cloned.1.call-start = ((), (), s32[]{:S(2)}) async-start(), calls=%async_computation.4 | async-start | bytes 5013504 | tf_op jit(solution)/shard_map/all_gather | solution.py:132
  101.7 529.6 %all-gather.21.cloned.1.call-start = ((), (), s32[]{:S(2)}) async-start(), calls=%async_computation.5 | async-start | bytes 5013504 | tf_op jit(solution)/shard_map/all_gather | solution.py:133
  102.3 581.2 %reduce-scatter.7.cloned.1.call-start = ((), (), s32[]{:S(2)}) async-start(), calls=%async_computation.12 | async-start | bytes 1769472
  104.5 320.5 %copy-start.20 = (s32[1024]{0:T(1024)}, s32[1024]{0:T(1024)S(1)}, u32[]{:S(2)}) copy-start(s32[1024]{0:T(1024)S(1)} %pad_clamp_fusion) | copy-start | bytes 12292
  434.2 4.7 copy-start.5
  440.3 4.7 copy-start.19
  445.0 1.0 copy-start.25
  446.0 1.2 copy-start.4
  447.3 1.1 copy-start.15
  448.1 1.5 copy-start.8
  639.8 44.8 %copy-start.2 = (s32[1,128,384]{2,1,0:T(8,128)S(1)}, s32[1,128,384]{2,1,0:T(8,128)}, u32[]{:S(2)}) copy-start(s32[1,128,384]{2,1,0:T(8,128)} %param.13) | copy-start | bytes 589828
  639.8 44.8 %copy-start.11 = (f32[128,384]{1,0:T(8,128)S(1)}, f32[128,384]{1,0:T(8,128)}, u32[]{:S(2)}) copy-start(f32[128,384]{1,0:T(8,128)} %param.12) | copy-start | bytes 589828
  639.8 44.9 %copy-start.27 = (f32[128]{0:T(128)S(1)}, f32[128]{0:T(128)}, u32[]{:S(2)}) copy-start(f32[128]{0:T(128)} %copy-done.26) | copy-start | bytes 1540
  639.9 211.8 %all-gather.31.cloned.1.call-start = ((), (), s32[]{:S(2)}) async-start(), calls=%async_computation.10 | async-start | bytes 1671168 | tf_op jit(solution)/shard_map/all_gather | solution.py:152
  684.6 63.6 %copy-start.14 = (f32[256,384]{1,0:T(8,128)}, f32[256,384]{1,0:T(8,128)S(1)}, u32[]{:S(2)}) copy-start(f32[256,384]{1,0:T(8,128)S(1)} %convert_element_type.128) | copy-start | bytes 1179652
  684.8 63.5 %copy-start.12 = (f32[128,384]{1,0:T(8,128)}, f32[128,384]{1,0:T(8,128)S(1)}, u32[]{:S(2)}) copy-start(f32[128,384]{1,0:T(8,128)S(1)} %get-tuple-element.23) | copy-start | bytes 589828
  748.3 6.8 copy-start.18
  755.9 177.3 %all-gather.33.cloned.1.call-start = ((), (), s32[]{:S(2)}) async-start(), calls=%async_computation.11 | async-start | bytes 1671168 | tf_op jit(solution)/shard_map/all_gather | solution.py:154
  756.6 257.9 %all-gather.25.cloned.1.call-start = ((), (), s32[]{:S(2)}) async-start(), calls=%async_computation.7 | async-start | bytes 1671168 | tf_op jit(solution)/shard_map/all_gather | solution.py:153
  758.6 0.7 copy-start.22
  761.1 335.0 %all-gather.23.cloned.1.call-start = ((), (), s32[]{:S(2)}) async-start(), calls=%async_computation.6 | async-start | bytes 1671168 | tf_op jit(solution)/shard_map/all_gather | solution.py:151
  761.8 412.0 %reduce-scatter.9.cloned.1.call-start = ((), (), s32[]{:S(2)}) async-start(), calls=%async_computation.13 | async-start | bytes 1769472
  762.0 6.2 copy-start.9
  762.0 6.4 slice-start
  763.8 4.7 slice-start.1
  1102.6 4.7 copy-start.6
  1117.9 0.9 copy-start.10
  1117.9 0.9 copy-start.24
  1118.9 1.1 copy-start.16
  1120.0 1.2 copy-start.3
  1121.2 1.1 copy-start.7
  1122.3 2.1 copy-start.1
  1129.3 45.6 %copy-start.13 = (f32[128,384]{1,0:T(8,128)S(1)}, f32[128,384]{1,0:T(8,128)}, u32[]{:S(2)}) copy-start(f32[128,384]{1,0:T(8,128)} %copy-done.12) | copy-start | bytes 589828
  1129.3 45.6 %copy-start.23 = (f32[384]{0:T(512)S(1)}, f32[384]{0:T(512)}, u32[]{:S(2)}) copy-start(f32[384]{0:T(512)} %get-tuple-element.15) | copy-start | bytes 4612
Sparse Core Ops, SparseCore 0:
  85.7 94.2 all-gather.26
  182.6 78.8 all-gather.28
  264.7 78.8 all-gather.16
  346.0 78.8 all-gather.14
  427.4 100.9 all-gather.18
  530.8 100.4 all-gather.20
  640.0 43.4 reduce-scatter.6
  756.0 95.6 all-gather.30
  854.3 78.8 all-gather.32
  935.6 78.8 all-gather.24
  1017.1 78.8 all-gather.22
  1129.4 44.2 reduce-scatter.8
